TPU v7x, 32 devices: a whole 2x2x4 slice. The times are simulated.
32 devices in a mesh: mesh: 8 (over z, y), pts: 4 (over x, core).
Axes of the slice: x: 2, y: 2, z: 4, core: 2. Of those that a mesh axis runs over, the one named last changes fastest.
Arguments:
- inputs: float32 [32768, 8], P(('mesh', 'pts')), may hold values from -6 to 6
- target: float32 [32768, 4], P(('mesh', 'pts')), may hold values from -6 to 6
- lengths: int32 [8, 4], P('mesh'), may hold values from 1 to 2048, 4096 in all within a row
- step_count: int32 [1], replicated, may hold values from 2 to 20
- muon_weight: float32 [2, 5, 256, 256], P(None, None, ('mesh', 'pts')), may hold values from -0.375 to 0.375
- muon_moment: float32 [2, 5, 256, 256], P(None, None, ('mesh', 'pts')), may hold values from -0.0017089844 to 0.0017089844
- adam_weight: float32 [18848], P(('mesh', 'pts'))
- adam_first: float32 [18848], P(('mesh', 'pts')), may hold values from -0.0004272461 to 0.0004272461
- adam_second: float32 [18848], P(('mesh', 'pts')), may hold values from 2e-11 to 4e-09
Outputs:
- new_muon_weight: float32 [2, 5, 256, 256], P(None, None, ('mesh', 'pts'))
- new_muon_moment: float32 [2, 5, 256, 256], P(None, None, ('mesh', 'pts'))
- new_adam_weight: float32 [18848], P(('mesh', 'pts'))
- new_adam_first: float32 [18848], P(('mesh', 'pts'))
- new_adam_second: float32 [18848], P(('mesh', 'pts'))
- step_loss: float32 [], replicated
- clip_norm: float32 [], replicated
Inputs may be any that keep to these rules, and one draw needn't show every extreme that they name: Each group's 4 lengths sum to 4096, and the largest of each group is exactly half of that.
All inputs are finite; a program needn't handle non-finite values.
Results may differ from a plain program's by a relative error of at most 0.0003.
Values sent between devices are 32-bit elements; how exact they have to be, the bound alone decides.
A program may use at most 192 MiB of HBM per device.

v0:
```python
from functools import partial
import math
import jax
import jax.numpy as jnp
from jax import lax
from jax.sharding import PartitionSpec as P

C = 256
H = 8
DH = 32
S = 64
IN = 8
OUT = 4
L = 2
HIGH = lax.Precision.HIGHEST
ns_a = 3.4445
ns_b = -4.775
ns_c = 2.0315
peak_rate = 0.3
warm_steps = 12.0
total_steps = 40.0


def layout():
    pieces = [
        ("emb_w", (IN, C)),
        ("emb_b", (C,)),
        ("head_w", (C, OUT)),
        ("head_b", (OUT,)),
        ("fin", (2, C)),
        ("qkv", (L, 3, DH, DH)),
        ("slice_w", (L, DH, S)),
        ("slice_b", (L, S)),
        ("temp", (L, H)),
        ("vec", (L, 9, C)),
    ]
    places = {}
    offset = 0
    for label_text, extent in pieces:
        places[label_text] = (offset, extent)
        offset = offset + math.prod(extent)
    return places


def unpack(packed):
    return {
        label_text: packed[offset : offset + math.prod(extent)].reshape(extent)
        for label_text, (offset, extent) in layout().items()
    }


def matmul(left, right):
    return jnp.dot(left, right, precision=HIGH)


def norm_rows(values, gain, shift):
    centre = values - jnp.mean(values, axis=-1, keepdims=True)
    spread = jnp.mean(centre * centre, axis=-1, keepdims=True)
    return centre * lax.rsqrt(spread + 1e-05) * gain + shift


def mesh_mask(lengths_row, first, points):
    ends = jnp.cumsum(lengths_row)
    starts = ends - lengths_row
    position = first + jnp.arange(points, dtype=jnp.int32)
    inside = (position[:, None] >= starts[None, :]) & (position[:, None] < ends[None, :])
    return inside.astype(jnp.float32)


def embed_piece(inputs, packed):
    params = unpack(packed)
    return matmul(inputs, params["emb_w"]) + params["emb_b"]


def slice_piece(hidden, matrices, packed, layer_index, onehot):
    params = unpack(packed)
    vectors = params["vec"][layer_index]
    points = hidden.shape[0]
    normed = norm_rows(hidden, vectors[0], vectors[1])
    features = (matmul(normed, matrices[0]) + vectors[2]).reshape(points, H, DH)
    routed = (matmul(normed, matrices[1]) + vectors[3]).reshape(points, H, DH)
    logits = jnp.einsum("phd,ds->phs", routed, params["slice_w"][layer_index], precision=HIGH)
    logits = (logits + params["slice_b"][layer_index]) / params["temp"][layer_index][:, None]
    weights = jax.nn.softmax(logits, axis=-1)
    numerator = jnp.einsum("pm,phs,phd->mhsd", onehot, weights, features, precision=HIGH)
    denominator = jnp.einsum("pm,phs->mhs", onehot, weights, precision=HIGH)
    return (weights, numerator, denominator)


def mix_piece(numerator, denominator, packed, layer_index):
    triple = unpack(packed)["qkv"][layer_index]
    tokens = numerator / (denominator[..., None] + 1e-05)
    queries = jnp.einsum("mhsd,de->mhse", tokens, triple[0], precision=HIGH)
    keys_all = jnp.einsum("mhsd,de->mhse", tokens, triple[1], precision=HIGH)
    values = jnp.einsum("mhsd,de->mhse", tokens, triple[2], precision=HIGH)
    scores = jnp.einsum("mhsd,mhtd->mhst", queries, keys_all, precision=HIGH) * DH ** (-0.5)
    return jnp.einsum("mhst,mhtd->mhsd", jax.nn.softmax(scores, axis=-1), values, precision=HIGH)


def out_piece(hidden, weights, mixed, matrices, packed, layer_index, onehot):
    vectors = unpack(packed)["vec"][layer_index]
    points = hidden.shape[0]
    spread_wts = onehot[:, :, None, None] * weights[:, None, :, :]
    pointwise = jnp.einsum("pmhs,mhsd->phd", spread_wts, mixed, precision=HIGH).reshape(points, C)
    hidden = hidden + matmul(pointwise, matrices[2]) + vectors[4]
    normed = norm_rows(hidden, vectors[5], vectors[6])
    inner = jax.nn.gelu(matmul(normed, matrices[3]) + vectors[7], approximate=False)
    return hidden + matmul(inner, matrices[4]) + vectors[8]


def head_piece(hidden, packed, target, onehot):
    params = unpack(packed)
    normed = norm_rows(hidden, params["fin"][0], params["fin"][1])
    predicted = matmul(normed, params["head_w"]) + params["head_b"]
    misfit = predicted - target
    errors = matmul(onehot.T, jnp.sum(misfit * misfit, axis=-1))
    scales = matmul(onehot.T, jnp.sum(target * target, axis=-1))
    return (errors, scales)


def loss_piece(errors, scales, meshes, floor_value):
    return jnp.sum(jnp.sqrt((errors + 1e-06) / jnp.maximum(scales, floor_value))) / meshes


def one_cycle(count):
    start_rate = peak_rate / 25.0
    end_rate = start_rate / 10000.0
    rising = start_rate + (peak_rate - start_rate) * 0.5 * (
        1.0 - jnp.cos(math.pi * count / warm_steps)
    )
    falling = end_rate + (peak_rate - end_rate) * 0.5 * (
        1.0 + jnp.cos(math.pi * (count - warm_steps) / (total_steps - warm_steps))
    )
    return jnp.where(count <= warm_steps, rising, falling)


def newton_schulz(current, gram_of):
    for sweep in range(5):
        gram = gram_of(current)
        product = jnp.einsum("...rc,...cd->...rd", current, gram, precision=HIGH)
        current = (
            ns_a * current
            + ns_b * product
            + ns_c * jnp.einsum("...rc,...cd->...rd", product, gram, precision=HIGH)
        )
    return current


def apply_update(
    grad_muon,
    grad_adam,
    square_sum,
    step_count,
    muon_weight,
    muon_moment,
    adam_weight,
    adam_first,
    adam_second,
    frob_of,
    orthogonal_of,
):
    norm_value = jnp.sqrt(square_sum)
    factor = 0.1 / jnp.maximum(norm_value, 0.1)
    moment = 0.95 * muon_moment + factor * grad_muon
    normalized = moment / (jnp.sqrt(frob_of(moment)) + 1e-07)[..., None, None]
    current = orthogonal_of(normalized)
    count = step_count[0].astype(jnp.float32)
    rate = one_cycle(count)
    new_muon = muon_weight * (1.0 - rate * 0.01) - rate * (0.2 * C**0.5) * current
    clipped = factor * grad_adam
    first = 0.9 * adam_first + 0.1 * clipped
    second = 0.999 * adam_second + 0.001 * clipped * clipped
    first_hat = first / (1.0 - 0.9**count)
    second_hat = second / (1.0 - 0.999**count)
    new_adam = adam_weight * (1.0 - rate * 0.01) - rate * first_hat / (jnp.sqrt(second_hat) + 1e-08)
    return (new_muon, moment, new_adam, first, second, norm_value)


def local(
    inputs,
    target,
    lengths,
    step_count,
    muon_weight,
    muon_moment,
    adam_weight,
    adam_first,
    adam_second,
):
    muon_all, adam_all = (
        lax.all_gather(muon_weight, ("mesh", "pts"), axis=2, tiled=True),
        lax.all_gather(adam_weight, ("mesh", "pts"), axis=0, tiled=True),
    )
    points = inputs.shape[0]
    pts_count = lax.axis_size("pts")
    floor_value = float(points * pts_count)
    onehot = mesh_mask(lengths[0], lax.axis_index("pts") * points, points)
    meshes = lax.axis_size("mesh") * lengths.shape[1]
    hidden, embed_back = jax.vjp(lambda packed: embed_piece(inputs, packed), adam_all)
    saved = []
    for layer_index in range(L):
        matrices = muon_all[layer_index]
        (weights, numerator, denominator), slice_back = jax.vjp(
            partial(slice_piece, layer_index=layer_index, onehot=onehot), hidden, matrices, adam_all
        )
        numerator, denominator = lax.psum((numerator, denominator), "pts")
        mixed, mix_back = jax.vjp(
            partial(mix_piece, layer_index=layer_index), numerator, denominator, adam_all
        )
        following, out_back = jax.vjp(
            partial(out_piece, layer_index=layer_index, onehot=onehot),
            hidden,
            weights,
            mixed,
            matrices,
            adam_all,
        )
        saved.append((slice_back, mix_back, out_back))
        hidden = following
    (errors, scales), head_back = jax.vjp(
        lambda state, packed: head_piece(state, packed, target, onehot), hidden, adam_all
    )
    errors, scales = lax.psum((errors, scales), "pts")
    group_loss, loss_back = jax.vjp(
        lambda first, second: loss_piece(first, second, meshes, floor_value), errors, scales
    )
    grad_errors, grad_scales = loss_back(jnp.ones_like(group_loss))
    grad_hidden, grad_adam = head_back((grad_errors, grad_scales))
    grad_layers = [None] * L
    for layer_index in reversed(range(L)):
        slice_back, mix_back, out_back = saved[layer_index]
        grad_hidden_out, grad_weights, grad_mixed, grad_mats_out, grad_adam_out = out_back(
            grad_hidden
        )
        grad_mixed = lax.psum(grad_mixed, "pts")
        grad_num, grad_den, grad_adam_mix = mix_back(grad_mixed)
        grad_hidden_in, grad_mats_in, grad_adam_in = slice_back((grad_weights, grad_num, grad_den))
        grad_hidden = grad_hidden_out + grad_hidden_in
        grad_adam = grad_adam + grad_adam_out + grad_adam_in + grad_adam_mix / pts_count
        grad_layers[layer_index] = grad_mats_out + grad_mats_in
    (grad_embed,) = embed_back(grad_hidden)
    grad_adam = grad_adam + grad_embed
    grad_muon = jnp.stack(grad_layers)
    grad_muon, grad_adam = (
        lax.psum_scatter(grad_muon, ("mesh", "pts"), scatter_dimension=2, tiled=True),
        lax.psum_scatter(grad_adam, ("mesh", "pts"), scatter_dimension=0, tiled=True),
    )
    square_sum, loss_total = lax.psum(
        (jnp.sum(grad_muon * grad_muon) + jnp.sum(grad_adam * grad_adam), group_loss / pts_count),
        ("mesh", "pts"),
    )

    def frob_of(moment):
        return lax.psum(jnp.sum(moment * moment, axis=(2, 3)), ("mesh", "pts"))

    def orthogonal_of(normalized):
        groups = lax.axis_size("mesh")
        count_all = normalized.shape[0] * normalized.shape[1]
        per_group = (count_all + groups - 1) // groups
        stacked = normalized.reshape((count_all,) + normalized.shape[2:])
        filler = jnp.zeros((per_group * groups - count_all,) + normalized.shape[2:], jnp.float32)
        spread = lax.all_to_all(
            jnp.concatenate([stacked, filler], axis=0),
            "mesh",
            split_axis=0,
            concat_axis=1,
            tiled=True,
        )

        def gram_of(current):
            return lax.psum(jnp.einsum("krc,krd->kcd", current, current, precision=HIGH), "pts")

        finished = newton_schulz(spread, gram_of)
        returned = lax.all_to_all(finished, "mesh", split_axis=1, concat_axis=0, tiled=True)
        return returned[:count_all].reshape(normalized.shape)

    results = apply_update(
        grad_muon,
        grad_adam,
        square_sum,
        step_count,
        muon_weight,
        muon_moment,
        adam_weight,
        adam_first,
        adam_second,
        frob_of,
        orthogonal_of,
    )
    return (results[0], results[1], results[2], results[3], results[4], loss_total, results[5])


def solution(mesh):
    in_specs = (
        P(("mesh", "pts"), None),
        P(("mesh", "pts"), None),
        P("mesh", None),
        P(),
        P(None, None, ("mesh", "pts"), None),
        P(None, None, ("mesh", "pts"), None),
        P(("mesh", "pts")),
        P(("mesh", "pts")),
        P(("mesh", "pts")),
    )
    out_specs = (
        P(None, None, ("mesh", "pts"), None),
        P(None, None, ("mesh", "pts"), None),
        P(("mesh", "pts")),
        P(("mesh", "pts")),
        P(("mesh", "pts")),
        P(),
        P(),
    )
    return jax.shard_map(local, mesh=mesh, in_specs=in_specs, out_specs=out_specs, check_vma=False)
```

profile of v0, /device:TPU:0, one launch (start us, length us, event | category | flops | bytes accessed | tf_op | source)
XLA Modules:
  0.0 1215.2 jit_solution(13003831298324453706)
XLA Ops:
  12.7 125.0 %all-reduce.100.cloned.1.call-done = f32[18848]{0:T(1024)} async-done(((f32[18848]{0:T(1024)}), f32[18848]{0:T(1024)}) %all-reduce.100.cloned.1.call-update) | async-done | bytes 75408
  154.3 45.1 %all-gather.2.cloned.1.call-done = f32[2,5,256,256]{3,2,1,0:T(8,128)} async-done(((f32[2,5,8,256]{3,2,1,0:T(8,128)}), f32[2,5,256,256]{3,2,1,0:T(8,128)}) %all-gather.2.cloned.1.call-update) | async-done | bytes 2621456 | tf_op jit(solution)/shard_map/all_gather | solution.py:191
  206.6 11.4 psum.113
  222.5 4.7 fusion.42
  229.9 29.6 %all-reduce.82.cloned.1.call-done = f32[4,8,64,32]{2,3,0,1:T(8,128)} async-done(((f32[4,8,64,32]{2,3,0,1:T(8,128)}), f32[4,8,64,32]{2,3,0,1:T(8,128)}) %all-reduce.82.cloned.1.call-update) | async-done | bytes 262160 | tf_op jit(solution)/shard_map/psum | solution.py:206
  267.9 5.2 fusion.2
  275.8 5.3 fusion.58
  291.5 10.1 psum.115
  306.2 4.7 fusion.47
  311.7 33.0 %all-reduce.84.cloned.1.call-done = f32[4,8,64,32]{2,3,0,1:T(8,128)} async-done(((f32[4,8,64,32]{2,3,0,1:T(8,128)}), f32[4,8,64,32]{2,3,0,1:T(8,128)}) %all-reduce.84.cloned.1.call-update) | async-done | bytes 262160 | tf_op jit(solution)/shard_map/psum | solution.py:206
  353.5 5.2 fusion
  361.3 5.4 fusion.59
  372.0 5.7 all-reduce.69
  412.6 12.3 %fusion.40 = f32[4,8,64,32]{2,3,0,1:T(8,128)} fusion(f32[8,32,1024,1]{2,1,3,0:T(8,128)S(1)} %convolution_bitcast_fusion.1, f32[1024,8,64]{0,2,1:T(8,128)S(1)} %copy-done.16, f32[1024,4]{0,1:T(4,128)S(1)} %copy-done.107), kind=kOutput, calls=%fused_computation.83 | convolution fusion | flops 807403520 | bytes 3424256 | tf_op jit(solution)/shard_map/transpose(jvp(pmhs,mhsd->phd))/dot_general | solution.py:104
  424.8 10.0 multiply_reduce_fusion.1
  444.8 23.6 %all-reduce.86.cloned.1.call-done = f32[4,8,64,32]{2,3,0,1:T(8,128)} async-done(((f32[4,8,64,32]{2,3,0,1:T(8,128)}), f32[4,8,64,32]{2,3,0,1:T(8,128)}) %all-reduce.86.cloned.1.call-update) | async-done | bytes 262160 | tf_op jit(solution)/shard_map/psum | solution.py:235
  480.6 4.8 fusion.13
  529.0 12.6 %fusion.41 = f32[4,8,64,32]{2,3,0,1:T(8,128)} fusion(f32[8,32,1024,1]{2,1,3,0:T(8,128)S(1)} %convolution_bitcast_fusion, f32[1024,8,64]{0,2,1:T(8,128)S(1)} %copy-done.9, f32[1024,4]{0,1:T(4,128)S(1)} %copy-done.109), kind=kOutput, calls=%fused_computation.84 | convolution fusion | flops 807403520 | bytes 3424256 | tf_op jit(solution)/shard_map/transpose(jvp(pmhs,mhsd->phd))/dot_general | solution.py:104
  541.7 9.7 multiply_reduce_fusion
  572.9 30.5 %all-reduce.88.cloned.1.call-done = f32[4,8,64,32]{2,3,0,1:T(8,128)} async-done(((f32[4,8,64,32]{2,3,0,1:T(8,128)}), f32[4,8,64,32]{2,3,0,1:T(8,128)}) %all-reduce.88.cloned.1.call-update) | async-done | bytes 262160 | tf_op jit(solution)/shard_map/psum | solution.py:235
  647.5 117.7 %all-reduce.102.cloned.1.call-done = f32[18848]{0:T(1024)} async-done(((f32[18848]{0:T(1024)}), f32[18848]{0:T(1024)}) %all-reduce.102.cloned.1.call-update) | async-done | bytes 75408
  766.6 142.6 %reduce-scatter.2.cloned.1.call-done = f32[2,5,8,256]{3,2,1,0:T(8,128)} async-done(((f32[2,5,256,256]{3,2,1,0:T(8,128)}), f32[2,5,8,256]{3,2,1,0:T(8,128)}) %reduce-scatter.2.cloned.1.call-update) | async-done | bytes 81936 | tf_op jit(solution)/shard_map/reduce_scatter | solution.py:245
  912.6 36.8 %psum.120 = f32[]{:T(128)} all-reduce(f32[]{:T(128)S(6)} %add.556), channel_id=1, replica_groups=mesh['mesh'=8,'pts'=4] {'mesh','pts'}, use_global_device_ids=true, to_apply=%region_77.78 | all-reduce | flops 1 | bytes 8 | tf_op jit(solution)/shard_map/psum | solution.py:248
  951.2 41.2 %all-reduce.68 = (f32[2,5]{1,0:T(2,128)S(1)}, f32[]{:T(128)}) all-reduce(f32[2,5]{1,0:T(2,128)S(1)} %get-tuple-element.29, f32[]{:T(128)S(6)} %div.387), channel_id=1, replica_groups=mesh['mesh'=8,'pts'=4] {'mesh','pts'}, use_global_device_ids=true, to_apply=%region_79.80 | all-reduce | flops 11 | bytes 88 | tf_op jit(solution)/shard_map/psum | solution.py:254
  992.5 11.9 all_to_all.33
  1005.9 31.6 %all-reduce.90.cloned.1.call-done = f32[2,256,256]{2,1,0:T(8,128)} async-done(((f32[2,256,256]{2,1,0:T(8,128)}), f32[2,256,256]{2,1,0:T(8,128)}) %all-reduce.90.cloned.1.call-update) | async-done | bytes 524304 | tf_op jit(solution)/shard_map/psum | solution.py:271
  1042.1 33.6 %all-reduce.92.cloned.1.call-done = f32[2,256,256]{2,1,0:T(8,128)} async-done(((f32[2,256,256]{2,1,0:T(8,128)}), f32[2,256,256]{2,1,0:T(8,128)}) %all-reduce.92.cloned.1.call-update) | async-done | bytes 524304 | tf_op jit(solution)/shard_map/psum | solution.py:271
  1080.2 33.6 %all-reduce.94.cloned.1.call-done = f32[2,256,256]{2,1,0:T(8,128)} async-done(((f32[2,256,256]{2,1,0:T(8,128)}), f32[2,256,256]{2,1,0:T(8,128)}) %all-reduce.94.cloned.1.call-update) | async-done | bytes 524304 | tf_op jit(solution)/shard_map/psum | solution.py:271
  1118.5 33.4 %all-reduce.96.cloned.1.call-done = f32[2,256,256]{2,1,0:T(8,128)} async-done(((f32[2,256,256]{2,1,0:T(8,128)}), f32[2,256,256]{2,1,0:T(8,128)}) %all-reduce.96.cloned.1.call-update) | async-done | bytes 524304 | tf_op jit(solution)/shard_map/psum | solution.py:271
  1156.4 33.7 %all-reduce.98.cloned.1.call-done = f32[2,256,256]{2,1,0:T(8,128)} async-done(((f32[2,256,256]{2,1,0:T(8,128)}), f32[2,256,256]{2,1,0:T(8,128)}) %all-reduce.98.cloned.1.call-update) | async-done | bytes 524304 | tf_op jit(solution)/shard_map/psum | solution.py:271
  1193.8 5.5 all-to-all-start.1
  1201.7 5.0 all-to-all-done.1
  (716 shorter events, 272.5 us)
Async XLA Ops:
  7.2 141.5 %copy-start = (f32[1024,8]{0,1:T(8,128)S(1)}, f32[1024,8]{0,1:T(8,128)}, u32[]{:S(2)}) copy-start(f32[1024,8]{0,1:T(8,128)} %param.9) | copy-start | bytes 98308
  7.2 130.6 %all-reduce.100.cloned.1.call-start = ((), (), s32[]{:S(2)}) async-start(), calls=%async_computation.14 | async-start | bytes 155648
  8.8 190.7 %all-gather.2.cloned.1.call-start = ((), (), s32[]{:S(2)}) async-start(), calls=%async_computation.3 | async-start | bytes 2703360 | tf_op jit(solution)/shard_map/all_gather | solution.py:191
  9.6 250.0 %all-reduce.82.cloned.1.call-start = ((), (), s32[]{:S(2)}) async-start(), calls=%async_computation.4 | async-start | bytes 1048576 | tf_op jit(solution)/shard_map/psum | solution.py:206
  10.4 279.7 %copy-start.153 = (s32[4,1]{0,1:T(1,128)}, s32[4,1]{0,1:T(1,128)S(1)}, u32[]{:S(2)}) copy-start(s32[4,1]{0,1:T(1,128)S(1)} %reduce-window.4) | copy-start | bytes 52
  11.8 278.3 %copy-start.156 = (s32[4]{0:T(128)}, s32[4]{0:T(128)S(1)}, u32[]{:S(2)}) copy-start(s32[4]{0:T(128)S(1)} %fusion.197) | copy-start | bytes 52
  11.9 189.8 %copy-start.192 = (pred[4,1024]{1,0:T(4,128)(4,1)}, pred[4,1024]{1,0:T(4,128)(4,1)S(1)}, u32[]{:S(2)}) copy-start(pred[4,1024]{1,0:T(4,128)(4,1)S(1)} %compare_and_fusion) | copy-start | bytes 12292
  12.7 340.4 %copy-start.106 = (f32[1024,4]{0,1:T(4,128)}, f32[1024,4]{0,1:T(4,128)S(1)}, u32[]{:S(2)}) copy-start(f32[1024,4]{0,1:T(4,128)S(1)} %fusion.222) | copy-start | bytes 49156
  146.4 139.7 %copy-start.129 = (f32[32,64,1]{1,0,2:T(8,128)}, f32[32,64,1]{1,0,2:T(8,128)S(1)}, u32[]{:S(2)}) copy-start(f32[32,64,1]{1,0,2:T(8,128)S(1)} %reshape.745) | copy-start | bytes 24580
  146.5 55.3 %copy-start.124 = (f32[32,64,1]{1,0,2:T(8,128)}, f32[32,64,1]{1,0,2:T(8,128)S(1)}, u32[]{:S(2)}) copy-start(f32[32,64,1]{1,0,2:T(8,128)S(1)} %reshape.738) | copy-start | bytes 24580
  148.6 70.6 %copy-start.137 = (f32[256]{0:T(256)}, f32[256]{0:T(256)S(1)}, u32[]{:S(2)}) copy-start(f32[256]{0:T(256)S(1)} %get-tuple-element.83) | copy-start | bytes 3076
  149.8 54.1 %copy-start.139 = (f32[1024]{0:T(1024)}, f32[1024]{0:T(1024)S(1)}, u32[]{:S(2)}) copy-start(f32[1024]{0:T(1024)S(1)} %multiply_reduce_fusion.22) | copy-start | bytes 12292
  151.2 53.2 %copy-start.175 = (f32[64]{0:T(128)}, f32[64]{0:T(128)S(1)}, u32[]{:S(2)}) copy-start(f32[64]{0:T(128)S(1)} %get-tuple-element.79) | copy-start | bytes 772
  152.6 51.9 %copy-start.177 = (f32[8]{0:T(128)}, f32[8]{0:T(128)S(1)}, u32[]{:S(2)}) copy-start(f32[8]{0:T(128)S(1)} %get-tuple-element.51) | copy-start | bytes 100
  154.3 65.0 %copy-start.147 = (f32[256]{0:T(256)}, f32[256]{0:T(256)S(1)}, u32[]{:S(2)}) copy-start(f32[256]{0:T(256)S(1)} %get-tuple-element.70) | copy-start | bytes 3076
  154.3 121.5 %copy-start.151 = (f32[256]{0:T(256)}, f32[256]{0:T(256)S(1)}, u32[]{:S(2)}) copy-start(f32[256]{0:T(256)S(1)} %get-tuple-element.66) | copy-start | bytes 3076
  154.3 148.6 %copy-start.135 = (f32[256]{0:T(256)}, f32[256]{0:T(256)S(1)}, u32[]{:S(2)}) copy-start(f32[256]{0:T(256)S(1)} %get-tuple-element.62) | copy-start | bytes 3076
  154.3 148.6 %copy-start.149 = (f32[256]{0:T(256)}, f32[256]{0:T(256)S(1)}, u32[]{:S(2)}) copy-start(f32[256]{0:T(256)S(1)} %get-tuple-element.61) | copy-start | bytes 3076
  205.3 62.6 %copy-start.8 = (f32[1024,8,64]{0,2,1:T(8,128)}, f32[1024,8,64]{0,2,1:T(8,128)S(1)}, u32[]{:S(2)}) copy-start(f32[1024,8,64]{0,2,1:T(8,128)S(1)} %fusion.36) | copy-start | bytes 6291460
  227.2 117.4 %all-reduce.84.cloned.1.call-start = ((), (), s32[]{:S(2)}) async-start(), calls=%async_computation.5 | async-start | bytes 1048576 | tf_op jit(solution)/shard_map/psum | solution.py:206
  310.9 157.6 %all-reduce.86.cloned.1.call-start = ((), (), s32[]{:S(2)}) async-start(), calls=%async_computation.6 | async-start | bytes 1048576 | tf_op jit(solution)/shard_map/psum | solution.py:235
  434.8 168.6 %all-reduce.88.cloned.1.call-start = ((), (), s32[]{:S(2)}) async-start(), calls=%async_computation.7 | async-start | bytes 1048576 | tf_op jit(solution)/shard_map/psum | solution.py:235
  569.8 195.4 %all-reduce.102.cloned.1.call-start = ((), (), s32[]{:S(2)}) async-start(), calls=%async_computation.15 | async-start | bytes 155648
  644.0 265.1 %reduce-scatter.2.cloned.1.call-start = ((), (), s32[]{:S(2)}) async-start(), calls=%async_computation.8 | async-start | bytes 2703360 | tf_op jit(solution)/shard_map/reduce_scatter | solution.py:245
  646.2 304.0 %copy-start.114 = (f32[2,5,8,256]{3,2,1,0:T(8,128)S(1)}, f32[2,5,8,256]{3,2,1,0:T(8,128)}, u32[]{:S(2)}) copy-start(f32[2,5,8,256]{3,2,1,0:T(8,128)} %param.14) | copy-start | bytes 245764
  646.3 391.3 %all-reduce.90.cloned.1.call-start = ((), (), s32[]{:S(2)}) async-start(), calls=%async_computation.9 | async-start | bytes 1048576 | tf_op jit(solution)/shard_map/psum | solution.py:271
  951.2 90.8 %copy-start.93 = (f32[2,5,8,256]{3,2,1,0:T(8,128)}, f32[2,5,8,256]{3,2,1,0:T(8,128)S(1)}, u32[]{:S(2)}) copy-start(f32[2,5,8,256]{3,2,1,0:T(8,128)S(1)} %get-tuple-element.30) | copy-start | bytes 245764
  1005.9 69.8 %all-reduce.92.cloned.1.call-start = ((), (), s32[]{:S(2)}) async-start(), calls=%async_computation.10 | async-start | bytes 1048576 | tf_op jit(solution)/shard_map/psum | solution.py:271
  1042.0 71.8 %all-reduce.94.cloned.1.call-start = ((), (), s32[]{:S(2)}) async-start(), calls=%async_computation.11 | async-start | bytes 1048576 | tf_op jit(solution)/shard_map/psum | solution.py:271
  1080.1 71.8 %all-reduce.96.cloned.1.call-start = ((), (), s32[]{:S(2)}) async-start(), calls=%async_computation.12 | async-start | bytes 1048576 | tf_op jit(solution)/shard_map/psum | solution.py:271
  1118.2 71.9 %all-reduce.98.cloned.1.call-start = ((), (), s32[]{:S(2)}) async-start(), calls=%async_computation.13 | async-start | bytes 1048576 | tf_op jit(solution)/shard_map/psum | solution.py:271
  1193.8 12.9 %all-to-all-start.1 = ((f32[2,64,256]{2,0,1:T(2,128)}), f32[2,64,256]{2,0,1:T(2,128)S(1)}, u32[]{:S(2)}, u32[]{:S(2)}) async-start(f32[2,64,256]{2,0,1:T(2,128)} %copy.325), calls=%async_computation.2 | async-start | bytes 262144 | tf_op jit(solution)/shard_map/all_to_all | solution.py:274
  (202 other events, 1190.0 us)
Sparse Core Ops, SparseCore 0:
  14.1 123.5 all-reduce.99
  140.6 58.7 all-gather.1
  227.3 32.1 all-reduce.81
  311.0 33.6 all-reduce.83
  435.0 33.4 all-reduce.85
  569.9 33.5 all-reduce.87
  644.2 120.9 all-reduce.101
  767.5 141.6 reduce-scatter.1
  1006.0 31.5 all-reduce.89
  1042.1 33.4 all-reduce.91
  1080.3 33.4 all-reduce.93
  1118.4 33.4 all-reduce.95
  1156.5 33.5 all-reduce.97
where the time goes:
time: 1220 us
  waiting for transfers between devices  719 us (59%)
  matrix products  250 us (20%)
  blocking collectives  117 us (10%)
  local copies, waits for them, and re-layouts  57.1 us (5%)
  other arithmetic  42.7 us (4%)
  between operations  22.1 us (2%)
    unnamed x15, waiting for transfers between devices  244 us
    psum x5, waiting for transfers between devices, gram_of(): lax.psum(jnp.einsum('krc,krd->kcd', current, current, precision=HIGH), 'p...  166 us
    reduce_scatter x1, waiting for transfers between devices, local(): lax.psum_scatter(grad_muon, ('mesh', 'pts'), scatter_dimension=2, tiled=T...  143 us
    dot_general x38, matrix products, matmul(): return jnp.dot(left, right, precision=HIGH)  87 us
    psum x2, waiting for transfers between devices, local(): numerator, denominator = lax.psum((numerator, denominator), 'pts')  62.6 us
    dot_general x6, matrix products, out_piece(): jnp.einsum('pmhs,mhsd->phd', spread_wts, mixed, precision=HIGH)  54.9 us
    psum x2, waiting for transfers between devices, local(): grad_mixed = lax.psum(grad_mixed, 'pts')  54.1 us
    all_gather x1, waiting for transfers between devices, local(): lax.all_gather(muon_weight, ('mesh', 'pts'), axis=2, tiled=True)  45.1 us
  transfers between devices with their start and end apart: 14, of which 14 were waited for; matrix products, arithmetic and copies ran while one was open for 3% of the time, Pallas kernels for 0%

commit v1 on v0

--- a/solution.py
+++ b/solution.py
@@ -19,6 +19,7 @@
 peak_rate = 0.3
 warm_steps = 12.0
 total_steps = 40.0
+open_strings_up = lambda z_in, which_axis: lax.all_gather(z_in, which_axis).sum(axis=0)
 
 
 def layout():
@@ -251,7 +252,7 @@
     )
 
     def frob_of(moment):
-        return lax.psum(jnp.sum(moment * moment, axis=(2, 3)), ("mesh", "pts"))
+        return open_strings_up(jnp.sum(moment * moment, axis=(2, 3)), ("mesh", "pts"))
 
     def orthogonal_of(normalized):
         groups = lax.axis_size("mesh")

time: 1220 us -> 1220 us (level)
    psum x1 -> x0, blocking collectives: 41.2 us -> none  [frob_of(): return lax.psum(jnp.sum(moment * moment, axis=(2, 3)), ('mesh', 'pts'))]
    all_gather x0 -> x1, blocking collectives: none -> 40 us  [lax.all_gather(z_in, which_axis).sum(axis=0)]
where the time goes in v1:
time: 1220 us; the launch traced here: 1210 us
  waiting for transfers between devices  717 us (59%)
  matrix products  250 us (20%)
  blocking collectives  114 us (9%)
  local copies, waits for them, and re-layouts  57.1 us (5%)
  other arithmetic  42.8 us (4%)
  between operations  22.1 us (2%)
    unnamed x15, waiting for transfers between devices  243 us
    psum x5, waiting for transfers between devices, gram_of(): lax.psum(jnp.einsum('krc,krd->kcd', current, current, precision=HIGH), 'p...  165 us
    reduce_scatter x1, waiting for transfers between devices, local(): lax.psum_scatter(grad_muon, ('mesh', 'pts'), scatter_dimension=2, tiled=T...  143 us
    dot_general x38, matrix products, matmul(): return jnp.dot(left, right, precision=HIGH)  87 us
    psum x2, waiting for transfers between devices, local(): numerator, denominator = lax.psum((numerator, denominator), 'pts')  62.6 us
    dot_general x6, matrix products, out_piece(): jnp.einsum('pmhs,mhsd->phd', spread_wts, mixed, precision=HIGH)  54.9 us
    psum x2, waiting for transfers between devices, local(): grad_mixed = lax.psum(grad_mixed, 'pts')  54.1 us
    all_gather x1, waiting for transfers between devices, local(): lax.all_gather(muon_weight, ('mesh', 'pts'), axis=2, tiled=True)  45.1 us
  transfers between devices with their start and end apart: 14, of which 14 were waited for; matrix products, arithmetic and copies ran while one was open for 3% of the time, Pallas kernels for 0%

profile of v1, /device:TPU:0, one launch (start us, length us, event | category | flops | bytes accessed | tf_op | source)
XLA Modules:
  0.0 1210.9 jit_solution(12038147257246657384)
XLA Ops:
  12.7 125.0 %all-reduce.100.cloned.1.call-done = f32[18848]{0:T(1024)} async-done(((f32[18848]{0:T(1024)}), f32[18848]{0:T(1024)}) %all-reduce.100.cloned.1.call-update) | async-done | bytes 75408
  154.3 45.1 %all-gather.4.cloned.1.call-done = f32[2,5,256,256]{3,2,1,0:T(8,128)} async-done(((f32[2,5,8,256]{3,2,1,0:T(8,128)}), f32[2,5,256,256]{3,2,1,0:T(8,128)}) %all-gather.4.cloned.1.call-update) | async-done | bytes 2621456 | tf_op jit(solution)/shard_map/all_gather | solution.py:192
  206.6 11.4 psum.106
  222.5 4.7 fusion.42
  229.9 29.6 %all-reduce.82.cloned.1.call-done = f32[4,8,64,32]{2,3,0,1:T(8,128)} async-done(((f32[4,8,64,32]{2,3,0,1:T(8,128)}), f32[4,8,64,32]{2,3,0,1:T(8,128)}) %all-reduce.82.cloned.1.call-update) | async-done | bytes 262160 | tf_op jit(solution)/shard_map/psum | solution.py:207
  267.9 5.2 fusion.2
  275.8 5.3 fusion.58
  291.5 10.1 psum.108
  306.2 4.7 fusion.47
  311.7 33.0 %all-reduce.84.cloned.1.call-done = f32[4,8,64,32]{2,3,0,1:T(8,128)} async-done(((f32[4,8,64,32]{2,3,0,1:T(8,128)}), f32[4,8,64,32]{2,3,0,1:T(8,128)}) %all-reduce.84.cloned.1.call-update) | async-done | bytes 262160 | tf_op jit(solution)/shard_map/psum | solution.py:207
  353.5 5.2 fusion
  361.3 5.4 fusion.59
  372.0 5.7 all-reduce.69
  412.6 12.3 %fusion.40 = f32[4,8,64,32]{2,3,0,1:T(8,128)} fusion(f32[8,32,1024,1]{2,1,3,0:T(8,128)S(1)} %convolution_bitcast_fusion.1, f32[1024,8,64]{0,2,1:T(8,128)S(1)} %copy-done.16, f32[1024,4]{0,1:T(4,128)S(1)} %copy-done.107), kind=kOutput, calls=%fused_computation.83 | convolution fusion | flops 807403520 | bytes 3424256 | tf_op jit(solution)/shard_map/transpose(jvp(pmhs,mhsd->phd))/dot_general | solution.py:105
  424.8 10.0 multiply_reduce_fusion.1
  444.8 23.6 %all-reduce.86.cloned.1.call-done = f32[4,8,64,32]{2,3,0,1:T(8,128)} async-done(((f32[4,8,64,32]{2,3,0,1:T(8,128)}), f32[4,8,64,32]{2,3,0,1:T(8,128)}) %all-reduce.86.cloned.1.call-update) | async-done | bytes 262160 | tf_op jit(solution)/shard_map/psum | solution.py:236
  480.6 4.8 fusion.13
  529.0 12.6 %fusion.41 = f32[4,8,64,32]{2,3,0,1:T(8,128)} fusion(f32[8,32,1024,1]{2,1,3,0:T(8,128)S(1)} %convolution_bitcast_fusion, f32[1024,8,64]{0,2,1:T(8,128)S(1)} %copy-done.9, f32[1024,4]{0,1:T(4,128)S(1)} %copy-done.109), kind=kOutput, calls=%fused_computation.84 | convolution fusion | flops 807403520 | bytes 3424256 | tf_op jit(solution)/shard_map/transpose(jvp(pmhs,mhsd->phd))/dot_general | solution.py:105
  541.7 9.7 multiply_reduce_fusion
  572.9 30.5 %all-reduce.88.cloned.1.call-done = f32[4,8,64,32]{2,3,0,1:T(8,128)} async-done(((f32[4,8,64,32]{2,3,0,1:T(8,128)}), f32[4,8,64,32]{2,3,0,1:T(8,128)}) %all-reduce.88.cloned.1.call-update) | async-done | bytes 262160 | tf_op jit(solution)/shard_map/psum | solution.py:236
  648.2 117.0 %all-reduce.102.cloned.1.call-done = f32[18848]{0:T(1024)} async-done(((f32[18848]{0:T(1024)}), f32[18848]{0:T(1024)}) %all-reduce.102.cloned.1.call-update) | async-done | bytes 75408
  766.6 142.6 %reduce-scatter.2.cloned.1.call-done = f32[2,5,8,256]{3,2,1,0:T(8,128)} async-done(((f32[2,5,256,256]{3,2,1,0:T(8,128)}), f32[2,5,8,256]{3,2,1,0:T(8,128)}) %reduce-scatter.2.cloned.1.call-update) | async-done | bytes 81936 | tf_op jit(solution)/shard_map/reduce_scatter | solution.py:246
  912.0 36.8 %all-reduce.68 = (f32[]{:T(128)}, f32[]{:T(128)}) all-reduce(f32[]{:T(128)S(6)} %add.558, f32[]{:T(128)S(6)} %div.387), channel_id=1, replica_groups=mesh['mesh'=8,'pts'=4] {'mesh','pts'}, use_global_device_ids=true, to_apply=%region_77.78 | all-reduce | flops 2 | bytes 16 | tf_op jit(solution)/shard_map/psum | solution.py:249
  950.6 40.0 %all-gather.1 = f32[32,2,5]{2,1,0:T(2,128)S(1)} all-gather(f32[1,2,5]{2,1,0:T(2,128)S(1)} %bitcast.520), channel_id=2, replica_groups=mesh['mesh'=8,'pts'=4] {'mesh','pts'}, dimensions={0}, use_global_device_ids=true | all-gather | bytes 1320 | tf_op jit(solution)/shard_map/all_gather | solution.py:22
  990.8 10.2 all_to_all.33
  1002.5 30.7 %all-reduce.90.cloned.1.call-done = f32[2,256,256]{2,1,0:T(8,128)} async-done(((f32[2,256,256]{2,1,0:T(8,128)}), f32[2,256,256]{2,1,0:T(8,128)}) %all-reduce.90.cloned.1.call-update) | async-done | bytes 524304 | tf_op jit(solution)/shard_map/psum | solution.py:272
  1037.7 33.6 %all-reduce.92.cloned.1.call-done = f32[2,256,256]{2,1,0:T(8,128)} async-done(((f32[2,256,256]{2,1,0:T(8,128)}), f32[2,256,256]{2,1,0:T(8,128)}) %all-reduce.92.cloned.1.call-update) | async-done | bytes 524304 | tf_op jit(solution)/shard_map/psum | solution.py:272
  1075.8 33.6 %all-reduce.94.cloned.1.call-done = f32[2,256,256]{2,1,0:T(8,128)} async-done(((f32[2,256,256]{2,1,0:T(8,128)}), f32[2,256,256]{2,1,0:T(8,128)}) %all-reduce.94.cloned.1.call-update) | async-done | bytes 524304 | tf_op jit(solution)/shard_map/psum | solution.py:272
  1114.1 33.4 %all-reduce.96.cloned.1.call-done = f32[2,256,256]{2,1,0:T(8,128)} async-done(((f32[2,256,256]{2,1,0:T(8,128)}), f32[2,256,256]{2,1,0:T(8,128)}) %all-reduce.96.cloned.1.call-update) | async-done | bytes 524304 | tf_op jit(solution)/shard_map/psum | solution.py:272
  1152.1 33.7 %all-reduce.98.cloned.1.call-done = f32[2,256,256]{2,1,0:T(8,128)} async-done(((f32[2,256,256]{2,1,0:T(8,128)}), f32[2,256,256]{2,1,0:T(8,128)}) %all-reduce.98.cloned.1.call-update) | async-done | bytes 524304 | tf_op jit(solution)/shard_map/psum | solution.py:272
  1189.5 5.5 all-to-all-start.1
  1197.4 5.0 all-to-all-done.1
  (717 shorter events, 272.6 us)
Async XLA Ops:
  7.2 141.5 %copy-start = (f32[1024,8]{0,1:T(8,128)S(1)}, f32[1024,8]{0,1:T(8,128)}, u32[]{:S(2)}) copy-start(f32[1024,8]{0,1:T(8,128)} %param.9) | copy-start | bytes 98308
  7.2 130.6 %all-reduce.100.cloned.1.call-start = ((), (), s32[]{:S(2)}) async-start(), calls=%async_computation.14 | async-start | bytes 155648
  8.8 190.7 %all-gather.4.cloned.1.call-start = ((), (), s32[]{:S(2)}) async-start(), calls=%async_computation.3 | async-start | bytes 2703360 | tf_op jit(solution)/shard_map/all_gather | solution.py:192
  9.6 250.0 %all-reduce.82.cloned.1.call-start = ((), (), s32[]{:S(2)}) async-start(), calls=%async_computation.4 | async-start | bytes 1048576 | tf_op jit(solution)/shard_map/psum | solution.py:207
  10.4 279.7 %copy-start.153 = (s32[4,1]{0,1:T(1,128)}, s32[4,1]{0,1:T(1,128)S(1)}, u32[]{:S(2)}) copy-start(s32[4,1]{0,1:T(1,128)S(1)} %reduce-window.4) | copy-start | bytes 52
  11.8 278.3 %copy-start.156 = (s32[4]{0:T(128)}, s32[4]{0:T(128)S(1)}, u32[]{:S(2)}) copy-start(s32[4]{0:T(128)S(1)} %fusion.197) | copy-start | bytes 52
  11.9 189.8 %copy-start.192 = (pred[4,1024]{1,0:T(4,128)(4,1)}, pred[4,1024]{1,0:T(4,128)(4,1)S(1)}, u32[]{:S(2)}) copy-start(pred[4,1024]{1,0:T(4,128)(4,1)S(1)} %compare_and_fusion) | copy-start | bytes 12292
  12.7 340.4 %copy-start.106 = (f32[1024,4]{0,1:T(4,128)}, f32[1024,4]{0,1:T(4,128)S(1)}, u32[]{:S(2)}) copy-start(f32[1024,4]{0,1:T(4,128)S(1)} %fusion.222) | copy-start | bytes 49156
  146.4 139.7 %copy-start.129 = (f32[32,64,1]{1,0,2:T(8,128)}, f32[32,64,1]{1,0,2:T(8,128)S(1)}, u32[]{:S(2)}) copy-start(f32[32,64,1]{1,0,2:T(8,128)S(1)} %reshape.752) | copy-start | bytes 24580
  146.5 55.3 %copy-start.124 = (f32[32,64,1]{1,0,2:T(8,128)}, f32[32,64,1]{1,0,2:T(8,128)S(1)}, u32[]{:S(2)}) copy-start(f32[32,64,1]{1,0,2:T(8,128)S(1)} %reshape.745) | copy-start | bytes 24580
  148.6 70.6 %copy-start.137 = (f32[256]{0:T(256)}, f32[256]{0:T(256)S(1)}, u32[]{:S(2)}) copy-start(f32[256]{0:T(256)S(1)} %get-tuple-element.83) | copy-start | bytes 3076
  149.8 54.1 %copy-start.139 = (f32[1024]{0:T(1024)}, f32[1024]{0:T(1024)S(1)}, u32[]{:S(2)}) copy-start(f32[1024]{0:T(1024)S(1)} %multiply_reduce_fusion.22) | copy-start | bytes 12292
  151.2 53.2 %copy-start.175 = (f32[64]{0:T(128)}, f32[64]{0:T(128)S(1)}, u32[]{:S(2)}) copy-start(f32[64]{0:T(128)S(1)} %get-tuple-element.79) | copy-start | bytes 772
  152.6 51.9 %copy-start.177 = (f32[8]{0:T(128)}, f32[8]{0:T(128)S(1)}, u32[]{:S(2)}) copy-start(f32[8]{0:T(128)S(1)} %get-tuple-element.51) | copy-start | bytes 100
  154.3 65.0 %copy-start.147 = (f32[256]{0:T(256)}, f32[256]{0:T(256)S(1)}, u32[]{:S(2)}) copy-start(f32[256]{0:T(256)S(1)} %get-tuple-element.70) | copy-start | bytes 3076
  154.3 121.5 %copy-start.151 = (f32[256]{0:T(256)}, f32[256]{0:T(256)S(1)}, u32[]{:S(2)}) copy-start(f32[256]{0:T(256)S(1)} %get-tuple-element.66) | copy-start | bytes 3076
  154.3 148.6 %copy-start.135 = (f32[256]{0:T(256)}, f32[256]{0:T(256)S(1)}, u32[]{:S(2)}) copy-start(f32[256]{0:T(256)S(1)} %get-tuple-element.62) | copy-start | bytes 3076
  154.3 148.6 %copy-start.149 = (f32[256]{0:T(256)}, f32[256]{0:T(256)S(1)}, u32[]{:S(2)}) copy-start(f32[256]{0:T(256)S(1)} %get-tuple-element.61) | copy-start | bytes 3076
  205.3 62.6 %copy-start.8 = (f32[1024,8,64]{0,2,1:T(8,128)}, f32[1024,8,64]{0,2,1:T(8,128)S(1)}, u32[]{:S(2)}) copy-start(f32[1024,8,64]{0,2,1:T(8,128)S(1)} %fusion.36) | copy-start | bytes 6291460
  227.2 117.4 %all-reduce.84.cloned.1.call-start = ((), (), s32[]{:S(2)}) async-start(), calls=%async_computation.5 | async-start | bytes 1048576 | tf_op jit(solution)/shard_map/psum | solution.py:207
  310.9 157.6 %all-reduce.86.cloned.1.call-start = ((), (), s32[]{:S(2)}) async-start(), calls=%async_computation.6 | async-start | bytes 1048576 | tf_op jit(solution)/shard_map/psum | solution.py:236
  434.8 168.6 %all-reduce.88.cloned.1.call-start = ((), (), s32[]{:S(2)}) async-start(), calls=%async_computation.7 | async-start | bytes 1048576 | tf_op jit(solution)/shard_map/psum | solution.py:236
  569.8 195.4 %all-reduce.102.cloned.1.call-start = ((), (), s32[]{:S(2)}) async-start(), calls=%async_computation.15 | async-start | bytes 155648
  644.0 265.1 %reduce-scatter.2.cloned.1.call-start = ((), (), s32[]{:S(2)}) async-start(), calls=%async_computation.8 | async-start | bytes 2703360 | tf_op jit(solution)/shard_map/reduce_scatter | solution.py:246
  646.2 303.3 %copy-start.114 = (f32[2,5,8,256]{3,2,1,0:T(8,128)S(1)}, f32[2,5,8,256]{3,2,1,0:T(8,128)}, u32[]{:S(2)}) copy-start(f32[2,5,8,256]{3,2,1,0:T(8,128)} %param.14) | copy-start | bytes 245764
  646.3 386.9 %all-reduce.90.cloned.1.call-start = ((), (), s32[]{:S(2)}) async-start(), calls=%async_computation.9 | async-start | bytes 1048576 | tf_op jit(solution)/shard_map/psum | solution.py:272
  950.6 87.0 %copy-start.93 = (f32[2,5,8,256]{3,2,1,0:T(8,128)}, f32[2,5,8,256]{3,2,1,0:T(8,128)S(1)}, u32[]{:S(2)}) copy-start(f32[2,5,8,256]{3,2,1,0:T(8,128)S(1)} %get-tuple-element.30) | copy-start | bytes 245764
  1002.4 68.9 %all-reduce.92.cloned.1.call-start = ((), (), s32[]{:S(2)}) async-start(), calls=%async_computation.10 | async-start | bytes 1048576 | tf_op jit(solution)/shard_map/psum | solution.py:272
  1037.7 71.8 %all-reduce.94.cloned.1.call-start = ((), (), s32[]{:S(2)}) async-start(), calls=%async_computation.11 | async-start | bytes 1048576 | tf_op jit(solution)/shard_map/psum | solution.py:272
  1075.8 71.8 %all-reduce.96.cloned.1.call-start = ((), (), s32[]{:S(2)}) async-start(), calls=%async_computation.12 | async-start | bytes 1048576 | tf_op jit(solution)/shard_map/psum | solution.py:272
  1113.9 71.9 %all-reduce.98.cloned.1.call-start = ((), (), s32[]{:S(2)}) async-start(), calls=%async_computation.13 | async-start | bytes 1048576 | tf_op jit(solution)/shard_map/psum | solution.py:272
  1189.5 12.9 %all-to-all-start.1 = ((f32[2,64,256]{2,0,1:T(2,128)}), f32[2,64,256]{2,0,1:T(2,128)S(1)}, u32[]{:S(2)}, u32[]{:S(2)}) async-start(f32[2,64,256]{2,0,1:T(2,128)} %copy.325), calls=%async_computation.2 | async-start | bytes 262144 | tf_op jit(solution)/shard_map/all_to_all | solution.py:275
  (202 other events, 1190.0 us)
Sparse Core Ops, SparseCore 0:
  14.1 123.5 all-reduce.99
  140.6 58.7 all-gather.3
  227.3 32.1 all-reduce.81
  311.0 33.6 all-reduce.83
  435.0 33.4 all-reduce.85
  569.9 33.5 all-reduce.87
  644.2 120.9 all-reduce.101
  767.5 141.6 reduce-scatter.1
  1002.6 30.5 all-reduce.89
  1037.8 33.5 all-reduce.91
  1075.9 33.4 all-reduce.93
  1114.0 33.4 all-reduce.95
  1152.2 33.5 all-reduce.97
